TPU v7x, 8 devices: a whole 2x2x1 slice. The times are simulated.
8 devices in a mesh: dp: 2 (over z, y), emb: 4 (over x, core).
Axes of the slice: x: 2, y: 2, z: 1, core: 2. Of those that a mesh axis runs over, the one named last changes fastest.
Arguments:
- tok_ids: int32 [4096], P(('dp', 'emb'))
- resid_in: bfloat16 [4096, 3072], P(('dp', 'emb'))
- cot_out: bfloat16 [4096, 3072], P(('dp', 'emb'))
- tables: bfloat16 [4, 128256, 256], P(None, 'emb')
- w_up: bfloat16 [4, 3072, 8192], replicated
- w_down: bfloat16 [4, 8192, 3072], replicated
- w_gate: bfloat16 [4, 3072, 256], replicated
- w_proj: bfloat16 [4, 256, 3072], replicated
Outputs:
- output 1: bfloat16 [4096, 3072], P(('dp', 'emb'))
- output 2: float32 [4, 128256, 256], P(None, 'emb')
All inputs are finite; a program needn't handle non-finite values.
Results may differ from a plain program's by a relative error of at most 0.0110832.
Values are sent between devices in bfloat16 or wider.
A program may use at most 2.5 GiB of HBM per device.

v0:
```python
import functools

import jax
import jax.numpy as jnp
from jax import lax
from jax.experimental import pallas as pl
from jax.experimental.pallas import tpu as pltpu
from jax.sharding import PartitionSpec as P

NORM_EPS = 1e-6
BF = jnp.bfloat16
F32 = jnp.float32
I32 = jnp.int32
VMEM_BYTES = 67043328
GELU_C = 0.7978845608028654
GELU_A = 0.044715

MESH_AXES = ('dp', 'emb')
CAP = 256


def gelu(x):
    return 0.5 * x * (1.0 + jnp.tanh(GELU_C * (x + GELU_A * (x * x * x))))


def gelu_slope(x):
    sq = x * x
    th = jnp.tanh(GELU_C * (x + GELU_A * (x * sq)))
    return 0.5 * (1.0 + th) + (0.5 * GELU_C) * x * (1.0 - th * th) * (1.0 + (3 * GELU_A) * sq)


def dot(a, b):
    return jnp.dot(a, b, preferred_element_type=F32)


def dot_t(a, b):
    return lax.dot_general(a, b, (((1,), (1,)), ((), ())), preferred_element_type=F32)


def row_loop(rows, slab, unroll=1):
    def run(body):
        def step(i, carry):
            body(pl.ds(pl.multiple_of(i * slab, slab), slab))
            return carry

        lax.fori_loop(0, rows // slab, step, 0, unroll=unroll)

    return run


def peer_of(n_emb, index):
    dp = index // n_emb
    return {'dp': dp, 'emb': index - dp * n_emb}


def remote(src, dst, send_sem, recv_sem, device):
    return pltpu.make_async_remote_copy(src_ref=src, dst_ref=dst, send_sem=send_sem, recv_sem=recv_sem,
                                        device_id=device, device_id_type=pl.DeviceIdType.MESH)


def meet(devices):
    barrier = pltpu.get_barrier_semaphore()
    for device in devices:
        pl.semaphore_signal(barrier, inc=1, device_id=device, device_id_type=pl.DeviceIdType.MESH)
    pl.semaphore_wait(barrier, len(devices))


def plan_kernel(cfg, in_ref, ids_ref, recv_ref, counts_ref, pick_ref, slot_row_ref, slot_col_ref, rank_s, send_sem, recv_sem):
    n_dp, n_emb, cap, range_rows, per_dot = cfg
    n_dev = n_dp * n_emb
    my_dp, my_emb = lax.axis_index('dp'), lax.axis_index('emb')
    me = my_dp * n_emb + my_emb
    n_sub, lanes = in_ref.shape
    tok = n_sub * lanes
    peers = [peer_of(n_emb, lax.rem(me + k, n_dev)) for k in range(1, n_dev)]
    meet(peers)
    copies = [remote(in_ref, ids_ref.at[me], send_sem.at[k], recv_sem.at[k], peer) for k, peer in enumerate(peers)]
    start(copies)
    ids_ref[me] = in_ref[...]

    def line(ref):
        return jnp.concatenate([ref[..., j, :] for j in range(n_sub)], axis=-1)

    def ones(cond):
        return jnp.where(cond, 1.0, 0.0)

    def digits(x):
        return jnp.concatenate([jnp.right_shift(x, 8), jnp.bitwise_and(x, 255)], axis=0).astype(F32).astype(BF)

    square = (tok, tok)
    down, right = lax.broadcasted_iota(I32, square, 0), lax.broadcasted_iota(I32, square, 1)
    earlier = ones(down < right).astype(BF)
    own = jnp.broadcast_to(jnp.concatenate([in_ref[j:j + 1, :] for j in range(n_sub)], axis=-1), (8, tok))
    owner = sum(jnp.where(own >= e * range_rows, 1, 0) for e in range(1, n_emb))
    is_owner = owner == lax.broadcasted_iota(I32, (8, tok), 0)
    own_rank = dot(ones(is_owner).astype(BF), earlier).astype(I32)
    slot_row = jnp.sum(jnp.where(is_owner, own_rank + owner * cap, 0).astype(F32), axis=0, keepdims=True).astype(I32)
    slot_row_ref[...] = slot_row
    turned = dot_t(ones(down == right).astype(BF), digits(jnp.broadcast_to(slot_row, (8, tok))))
    slot_col_ref[...] = (turned[:, 0:1] * 256.0 + turned[:, 8:9]).astype(I32)

    wait(copies)
    ids8 = line(ids_ref)
    low = my_emb * range_rows
    mine = jnp.logical_and(ids8 >= low, ids8 < low + range_rows)
    mine_f = ones(mine)
    rank_s[...] = jnp.where(mine, dot(mine_f.astype(BF), earlier), -1.0)
    counts = jnp.sum(mine_f, axis=1, keepdims=True).astype(I32)
    counts_ref[...] = jnp.broadcast_to(counts, counts_ref.shape)
    loc = digits(jnp.where(mine, ids8 - low, 0))
    c_iota = lax.broadcasted_iota(I32, (cap, tok), 0).astype(F32)
    dev_iota = lax.broadcasted_iota(I32, (n_dev, cap), 0)
    recv = jnp.zeros((n_dev, cap), F32)
    for d in range(n_dev):
        found = dot_t(loc, ones(rank_s[d:d + 1, :] == c_iota).astype(BF))
        recv = jnp.where(dev_iota == d, found[:n_dev] * 256.0 + found[n_dev:], recv)
    slot = dev_iota * cap + lax.broadcasted_iota(I32, (n_dev, cap), 1)
    recv_ref[...] = jnp.where(slot - dev_iota * cap < counts, recv.astype(I32), slot * 8)
    lane16 = lax.broadcasted_iota(I32, (cap, 2 * n_dev), 1)
    row1 = lax.broadcasted_iota(I32, (cap, 1), 0)
    for e in range(n_emb):
        d = my_dp * n_emb + e
        found = dot_t(ones(rank_s[pl.ds(d, 1), :] == c_iota).astype(BF), loc)
        low8 = jnp.sum(jnp.where(lane16 == n_dev + d, found, 0.0), axis=1, keepdims=True).astype(I32)
        pick_ref[e * cap:(e + 1) * cap, :] = jnp.bitwise_and(low8, 7) + 8 * jnp.bitwise_and(row1, per_dot - 1)


def gather_kernel(cfg, loc_ref, counts_ref, recv_ref, tally_ref, pick_ref, tables_hbm,
                  out_ref, dtab_hbm, read_ref, write_ref, group_ref, meta_ref, buf, zero_s, sems, z_sem):
    n_layers, n_dest, cap, per_dot, group, z_chunks, slot_bits = cfg
    trip = per_dot * group
    z_rows = zero_s.shape[0]
    first = lax.axis_index('dp') * n_dest
    n_trips = [(counts_ref[first + d, 0] + (trip - 1)) // trip for d in range(n_dest)]

    def row_copy(d, c):
        base = pl.multiple_of(jnp.left_shift(jnp.right_shift(loc_ref[first + d, c], 3), 3), 8)
        at = pl.multiple_of(d * cap * 8 + c * 8, 8)
        return pltpu.make_async_copy(tables_hbm.at[:, pl.ds(base, 8), :], buf.at[:, pl.ds(at, 8), :], sems.at[d])

    def z_copy(c):
        return pltpu.make_async_copy(zero_s, dtab_hbm.at[0, pl.ds(c * z_rows, z_rows)], z_sem)

    for d in range(n_dest):
        def issue(i, carry, d=d):
            for k in range(8):
                row_copy(d, i * 8 + k).start()
            return carry

        lax.fori_loop(0, n_trips[d] * (trip // 8), issue, 0)

    clear_rows(zero_s)

    def z_start(c, carry):
        z_copy(c).start(priority=1)
        return carry

    lax.fori_loop(0, z_chunks, z_start, 0)
    order_rows(recv_ref, tally_ref, slot_bits, read_ref, write_ref, group_ref, meta_ref)
    for d in range(n_dest):
        def drain(i, carry, d=d):
            part = buf.at[:, pl.ds(pl.multiple_of((d * cap + i * trip) * 8, 8), trip * 8), :]
            pltpu.make_async_copy(part, part, sems.at[d]).wait()
            return carry

        lax.fori_loop(0, n_trips[d], drain, 0)

        def pick(i, carry, d=d):
            for k in range(group):
                s0 = pl.multiple_of(d * cap + i * trip + k * per_dot, per_dot)
                want = pick_ref[pl.ds(s0, per_dot), :]
                sel = (lax.broadcasted_iota(I32, (per_dot, per_dot * 8), 1) == want).astype(BF)
                for l in range(n_layers):
                    rows = buf[l, pl.ds(pl.multiple_of(s0 * 8, 8), per_dot * 8), :]
                    out_ref[l, pl.ds(s0, per_dot), :] = dot(sel, rows).astype(BF)
            return carry

        lax.fori_loop(0, n_trips[d], pick, 0)

        def blank(i, carry, d=d):
            s0 = pl.multiple_of(d * cap + i * trip, trip)
            for l in range(n_layers):
                out_ref[l, pl.ds(s0, trip), :] = jnp.zeros((trip, out_ref.shape[2]), BF)
            return carry

        lax.fori_loop(n_trips[d], cap // trip, blank, 0)

    def z_wait(c, carry):
        z_copy(c).wait()
        return carry

    lax.fori_loop(0, z_chunks, z_wait, 0)


def clear_rows(ref):
    def clear(i, carry):
        ref[i] = jnp.zeros(ref.shape[1:], F32)
        return carry

    lax.fori_loop(0, ref.shape[0], clear, 0)


def weight_copies(wu_hbm, wd_hbm, wu_s, wd_s, sems):
    fb = wu_s.shape[2]

    def copies(layer, blk, slot):
        at = pl.multiple_of(blk * fb, fb)
        return (pltpu.make_async_copy(wu_hbm.at[layer, :, pl.ds(at, fb)], wu_s.at[slot], sems.at[0, slot]),
                pltpu.make_async_copy(wd_hbm.at[layer, pl.ds(at, fb), :], wd_s.at[slot], sems.at[1, slot]))

    return copies


def start(copies):
    for copy in copies:
        copy.start()


def wait(copies):
    for copy in copies:
        copy.wait()


def mlp_block(cfg, u_s, h_s, acc_s, wu_ref, wd_ref, up_ref, second=None):
    cw, nw = cfg
    gw = 128
    n_c = wu_ref.shape[1] // cw

    def act(c):
        for g in range(cw // gw):
            gs = slice(c * cw + g * gw, c * cw + (g + 1) * gw)
            h_s[:, gs] = gelu(up_ref[:, gs]).astype(BF)

    for c in range(n_c):
        cs = slice(c * cw, (c + 1) * cw)
        up_ref[:, cs] = dot(u_s[...], wu_ref[:, cs])
        if c > 0:
            act(c - 1)
    if second is not None:
        second.wait()
    for c in range(n_c):
        cs = slice(c * cw, (c + 1) * cw)
        for n in range(acc_s.shape[1] // nw):
            ns = slice(n * nw, (n + 1) * nw)
            acc_s[:, ns] += dot(h_s[:, cs], wd_ref[cs, ns])
        if c == 0:
            act(n_c - 1)


def norm_rows(x, sl, u_s, acc_s, scale_ref=None):
    scale = lax.rsqrt(jnp.mean(x * x, axis=-1, keepdims=True) + NORM_EPS)
    u_s[sl, :] = (x * scale).astype(BF)
    acc_s[sl, :] = x
    if scale_ref is not None:
        scale_ref[sl, :] = jnp.broadcast_to(scale, (scale.shape[0], scale_ref.shape[1]))


def add_proj(nw, acc_s, mixed, wp_ref):
    for n in range(acc_s.shape[1] // nw):
        ns = slice(n * nw, (n + 1) * nw)
        acc_s[:, ns] += dot(mixed, wp_ref[:, ns])


def first_kernel(cfg, x_hbm, slot_hbm, served_hbm, wg_hbm, wp_hbm, wu_hbm, wd_hbm,
                 x_out_hbm, gate_hbm, fet_hbm,
                 x_s, slot_s, gate_s, fet_s, u_s, acc_s, h_s, up_s, ret_s, wu_s, wd_s, wg_s, wp_s,
                 in_sem, out_sem, w_sem, self_sem, send_sem, recv_sem):
    n_dp, n_emb, cap, n_blk, cw, nw, slab = cfg
    tok, dim = u_s.shape
    my_emb = lax.axis_index('emb')
    my_dp = lax.axis_index('dp')
    here = ret_s.at[:, pl.ds(pl.multiple_of(my_emb * cap, cap), cap), :]
    own = pltpu.make_async_copy(served_hbm.at[:, pl.ds(pl.multiple_of(my_emb * cap, cap), cap), :], here, self_sem)
    peers = [lax.rem(my_emb + k, n_emb) for k in range(1, n_emb)]
    copies = [remote(served_hbm.at[:, pl.ds(pl.multiple_of(p * cap, cap), cap), :], here,
                     send_sem.at[k], recv_sem.at[k], {'dp': my_dp, 'emb': p}) for k, p in enumerate(peers)]
    weights = weight_copies(wu_hbm, wd_hbm, wu_s, wd_s, w_sem)
    first = [pltpu.make_async_copy(x_hbm, x_s, in_sem.at[0]),
             pltpu.make_async_copy(wg_hbm.at[0], wg_s, in_sem.at[1]),
             pltpu.make_async_copy(wp_hbm.at[0], wp_s, in_sem.at[2]),
             pltpu.make_async_copy(slot_hbm, slot_s, in_sem.at[3])]
    start(first[:2])
    start(weights(0, 0, 0))
    start(first[2:])
    meet([{'dp': my_dp, 'emb': p} for p in peers])
    own.start()
    start(copies)
    first[0].wait()
    row_loop(tok, slab)(lambda sl: norm_rows(x_s[sl, :].astype(F32), sl, u_s, acc_s))
    first[1].wait()
    gate_s[0] = dot(u_s[...], wg_s[...])
    gate_out = pltpu.make_async_copy(gate_s, gate_hbm, out_sem.at[0])
    gate_out.start()

    def block(f, carry):
        slot = lax.rem(f, 2)

        @pl.when(f + 1 < n_blk)
        def _():
            start(weights(0, f + 1, 1 - slot))

        up_w, down_w = weights(0, f, slot)
        up_w.wait()
        mlp_block((cw, nw), u_s, h_s, acc_s, wu_s.at[slot], wd_s.at[slot], up_s, down_w)
        return carry

    lax.fori_loop(0, n_blk, block, 0)
    own.wait()
    wait(copies)
    wait(first[2:])
    sel = (lax.broadcasted_iota(I32, (tok, n_emb * cap), 1) == slot_s[...]).astype(BF)
    for l in range(fet_s.shape[0]):
        fet_s[l] = dot(sel, ret_s[l]).astype(BF)
    add_proj(nw, acc_s, (gelu(gate_s[0]) * fet_s[0].astype(F32)).astype(BF), wp_s)
    fet_out = pltpu.make_async_copy(fet_s, fet_hbm, out_sem.at[1])
    fet_out.start()
    outs = []
    for half in range(2):
        rows = pl.ds(half * (tok // 2), tok // 2)

        def finish(sl, half=half):
            sl = pl.ds(sl.start + half * (tok // 2), slab)
            x_s[sl, :] = acc_s[sl, :].astype(BF)

        row_loop(tok // 2, slab)(finish)
        outs.append(pltpu.make_async_copy(x_s.at[rows], x_out_hbm.at[rows], out_sem.at[2 + half]))
        outs[-1].start()
    gate_out.wait()
    fet_out.wait()
    wait(outs)


def forward_kernel(cfg, x_hbm, cot_hbm, fet_hbm, wg_hbm, wp_hbm, wu_hbm, wd_hbm, dt_in,
                   out_hbm, saved_hbm, ups_hbm, gate_hbm, rows_hbm, dgp_hbm, dtab_hbm, scale_hbm,
                   x_s, u_s, acc_s, h_s, up_s, zero_s, fet_ref, gate_ref, rows_ref, dgp_ref, scale_ref, wu_s, wd_s, wg_s, wp_s,
                   in_sem, w_sem, up_sem, out_sem, z_sem):
    n_layers, n_blk, cw, nw, slab, z_per, z_chunks = cfg
    tok, dim = x_s.shape
    fb = wu_s.shape[2]
    z_rows = zero_s.shape[0]
    n_steps = n_layers * n_blk
    weights = weight_copies(wu_hbm, wd_hbm, wu_s, wd_s, w_sem)

    def z_copies(step):
        found = []
        for j in range(z_per):
            c = step * z_per + j
            zl = c // z_chunks
            found.append(pltpu.make_async_copy(zero_s, dtab_hbm.at[zl + 1, pl.ds((c - zl * z_chunks) * z_rows, z_rows)], z_sem.at[j]))
        return found

    def up_copy(layer, blk, slot):
        return pltpu.make_async_copy(up_s.at[slot], ups_hbm.at[layer, :, pl.ds(pl.multiple_of(blk * fb, fb), fb)], up_sem.at[slot])

    def gate_copy(layer):
        return pltpu.make_async_copy(wg_hbm.at[layer + 1], wg_s, in_sem.at[1])

    def proj_copy(layer):
        return pltpu.make_async_copy(wp_hbm.at[layer + 1], wp_s, in_sem.at[2])

    fetch = pltpu.make_async_copy(x_hbm, x_s, in_sem.at[0])
    fetch.start()
    gate_copy(0).start()
    start(weights(1, 0, 0))
    proj_copy(0).start()
    get_fet = pltpu.make_async_copy(fet_hbm, fet_ref, in_sem.at[3])
    get_fet.start()
    put_scales = pltpu.make_async_copy(scale_ref, scale_hbm, out_sem.at[1])

    def put_gate(layer):
        return pltpu.make_async_copy(gate_ref.at[layer], gate_hbm.at[layer], out_sem.at[2])

    clear_rows(zero_s)
    fetch.wait()
    row_loop(tok, slab)(lambda sl: norm_rows(x_s[sl, :].astype(F32), sl, u_s, acc_s, scale_ref.at[0]))

    def one_layer(layer, carry):
        gate_copy(layer).wait()
        gate_ref[layer] = dot(u_s[...], wg_s[...])
        put_gate(layer).start()

        @pl.when(layer == n_layers - 1)
        def _():
            put_scales.start()

        @pl.when(layer + 1 < n_layers)
        def _():
            gate_copy(layer + 1).start()

        def block(f, carry):
            step = layer * n_blk + f
            slot = lax.rem(step, 2)

            @pl.when(step + 1 < n_steps)
            def _():
                nxt = step + 1
                start(weights(1 + nxt // n_blk, lax.rem(nxt, n_blk), 1 - slot))

            @pl.when(step > 0)
            def _():
                wait(z_copies(step - 1))

            for copy in z_copies(step):
                copy.start(priority=1)

            @pl.when(step > 1)
            def _():
                up_copy(layer, f, slot).wait()

            wait(weights(1 + layer, f, slot))
            mlp_block((cw, nw), u_s, h_s, acc_s, wu_s.at[slot], wd_s.at[slot], up_s.at[slot])
            up_copy(layer, f, slot).start()
            return carry

        lax.fori_loop(0, n_blk, block, 0)
        proj_copy(layer).wait()
        put_gate(layer).wait()

        @pl.when(layer == 0)
        def _():
            get_fet.wait()

        add_proj(nw, acc_s, (gelu(gate_ref[layer]) * fet_ref[layer + 1].astype(F32)).astype(BF), wp_s)

        @pl.when(layer > 0)
        def _():
            pltpu.make_async_copy(x_s, saved_hbm.at[layer - 1], out_sem.at[0]).wait()

        def next_rows(sl):
            x_new = acc_s[sl, :].astype(BF)
            x_s[sl, :] = x_new
            norm_rows(x_new.astype(F32), sl, u_s, acc_s, scale_ref.at[jnp.minimum(layer + 1, n_layers - 1)])

        def last_rows(sl):
            x_s[sl, :] = acc_s[sl, :].astype(BF)

        @pl.when(layer < n_layers - 1)
        def _():
            row_loop(tok, slab)(next_rows)

        @pl.when(layer == n_layers - 1)
        def _():
            row_loop(tok, slab)(last_rows)

        @pl.when(layer < n_layers - 1)
        def _():
            pltpu.make_async_copy(x_s, saved_hbm.at[layer], out_sem.at[0]).start()
            proj_copy(layer + 1).start()

        return carry

    lax.fori_loop(0, n_layers, one_layer, 0)
    put = pltpu.make_async_copy(x_s, out_hbm, out_sem.at[0])
    put.start()
    get = pltpu.make_async_copy(cot_hbm, u_s, in_sem.at[0])
    get.start()
    wait(z_copies(n_steps - 1))
    up_copy(0, 0, 0).wait()
    up_copy(0, 0, 1).wait()
    get.wait()
    d_mixed = dot_t(u_s[...], wp_s[...]).astype(BF).astype(F32)
    gate_grads(gate_ref[n_layers - 1], fet_ref[n_layers], d_mixed, rows_ref, dgp_ref)
    small = [pltpu.make_async_copy(rows_ref, rows_hbm, out_sem.at[2]), pltpu.make_async_copy(dgp_ref, dgp_hbm, out_sem.at[3])]
    start(small)
    put_scales.wait()
    put.wait()
    wait(small)


def gate_grads(gate_pre, fetched, d_mixed, rows_ref, dgp_ref):
    rows_ref[...] = gelu(gate_pre) * d_mixed
    dgp_ref[...] = (d_mixed * fetched.astype(F32) * gelu_slope(gate_pre)).astype(BF)


def to_slots(rows, slot_ref, slots_s):
    hi = rows.astype(BF)
    rest = rows - hi.astype(F32)
    mid = rest.astype(BF)
    low = (rest - mid.astype(F32)).astype(BF)
    n = slots_s.shape[0] * slots_s.shape[2]
    sel = slot_pick(n, slot_ref)
    slots = (dot(sel, hi) + dot(sel, mid)) + dot(sel, low)
    for h in range(slots_s.shape[1]):
        slots_s[:, h] = slots[:, h * 128:(h + 1) * 128].reshape(n // 8, 8, 128)


def slot_pick(n, slot_ref):
    return (lax.broadcasted_iota(I32, (n, slot_ref.shape[1]), 0) == slot_ref[...]).astype(BF)


def backward_kernel(cfg, cot_hbm, x1_hbm, saved_hbm, rows_hbm, dgp_hbm, slot_hbm, gate0_hbm, gates_hbm, fet_hbm, scale_hbm,
                    ups_hbm, wu_hbm, wd_hbm, wg_hbm, wp_hbm,
                    got_hbm, gate_hbm, mixed_hbm,
                    cot_s, x_s, acc_s, dup_s, dh_s, dng_s, slots_s, gslots_s, dslots_s, rows_s, dgp_s, slot_ref, gate0_ref, gate_ref, fet_ref, scale_ref, up_s, wu_s, wd_s, wg_s, wp_s,
                    in_sem, w_sem, up_sem, send_sem, self_sem, recv_sem):
    n_layers, n_blk, n_dp, n_emb, cap, cw, nw, slab = cfg
    tok, dim = cot_s.shape
    fb = wu_s.shape[2]
    gw = 128
    n_dev = n_dp * n_emb
    n_steps = n_layers * n_blk
    my_emb = lax.axis_index('emb')
    me = lax.axis_index('dp') * n_emb + my_emb
    peers = [peer_of(n_emb, lax.rem(me + k, n_dev)) for k in range(1, n_dev)]
    weights = weight_copies(wu_hbm, wd_hbm, wu_s, wd_s, w_sem)

    def part(ref, emb):
        return ref.at[pl.ds(emb * (cap // 8), cap // 8)]

    def sends(ref, there, which, got):
        return [pltpu.make_async_copy(part(ref, my_emb), there, self_sem.at[which])] + [
            remote(part(ref, peer['emb']), there, send_sem.at[which, k], recv_sem.at[got, k], peer) for k, peer in enumerate(peers)]

    def row_sends(i):
        return sends(slots_s, part(got_hbm.at[n_layers - 1 - i], me), 0, i)

    gate_sends = sends(gslots_s, part(gate_hbm, me), 1, n_layers)

    def flat(ref, dev):
        return ref.at[pl.ds(pl.multiple_of(dev * cap, cap), cap), :]

    mixed_sends = [pltpu.make_async_copy(flat(dslots_s, my_emb), flat(mixed_hbm, me), self_sem.at[2])] + [
        remote(flat(dslots_s, peer['emb']), flat(mixed_hbm, me), send_sem.at[2, k], recv_sem.at[n_layers + 1, k], peer)
        for k, peer in enumerate(peers)]

    def up_copy(step, slot):
        i = step // n_blk
        blk = step - i * n_blk
        return pltpu.make_async_copy(ups_hbm.at[n_layers - 1 - i, :, pl.ds(pl.multiple_of(blk * fb, fb), fb)], up_s.at[slot], up_sem.at[slot])

    def load(step, slot):
        i = step // n_blk
        return weights(n_layers - i, step - i * n_blk, slot) + (up_copy(step, slot),)

    def gate_copy(i):
        return pltpu.make_async_copy(wg_hbm.at[n_layers - i], wg_s, in_sem.at[1])

    def proj_copy(i):
        return pltpu.make_async_copy(wp_hbm.at[n_layers - 1 - i], wp_s, in_sem.at[2])

    def x_copy(i):
        return pltpu.make_async_copy(saved_hbm.at[n_layers - 2 - i], x_s, in_sem.at[3])

    fetch = pltpu.make_async_copy(cot_hbm, cot_s, in_sem.at[0])
    soon = [pltpu.make_async_copy(src, dst, in_sem.at[4 + k]) for k, (src, dst) in enumerate(
        ((gate0_hbm, gate0_ref), (slot_hbm, slot_ref), (rows_hbm, rows_s), (dgp_hbm, dgp_s)))]
    later = [pltpu.make_async_copy(src, dst, in_sem.at[8 + k]) for k, (src, dst) in enumerate(
        ((gates_hbm, gate_ref), (fet_hbm, fet_ref), (scale_hbm, scale_ref)))]
    start(soon)
    gate_copy(0).start()
    fetch.start()
    start(load(0, 0))
    proj_copy(0).start()
    start(later)

    def clear(sl):
        acc_s[sl, :] = jnp.zeros((slab, dim), F32)

    row_loop(tok, slab)(clear)
    meet(peers)
    wait(soon)
    to_slots(gelu(gate0_ref[0]), slot_ref, gslots_s)

    def one_layer(i, carry):
        @pl.when(i < n_layers - 1)
        def _():
            x_copy(i).start()

        @pl.when(i == n_layers - 1)
        def _():
            pltpu.make_async_copy(x1_hbm, x_s, in_sem.at[3]).start()

        gate_copy(i).wait()
        to_slots(rows_s[...], slot_ref, slots_s)
        for n in range(dim // nw):
            ns = slice(n * nw, (n + 1) * nw)
            dng_s[:, ns] = dot_t(dgp_s[...], wg_s[ns, :]).astype(BF)
        start(row_sends(i))

        @pl.when(i < n_layers - 1)
        def _():
            gate_copy(i + 1).start()

        @pl.when(i == 0)
        def _():
            start(gate_sends)
            fetch.wait()

        def block(f, carry):
            step = i * n_blk + f
            slot = lax.rem(step, 2)

            @pl.when(step + 1 < n_steps)
            def _():
                start(load(step + 1, 1 - slot))

            wait(load(step, slot))
            wu_ref, wd_ref, up_ref = wu_s.at[slot], wd_s.at[slot], up_s.at[slot]

            def act(c):
                for g in range(cw // gw):
                    gs = slice(c * cw + g * gw, c * cw + (g + 1) * gw)
                    dup_s[:, gs] = (dh_s[:, gs].astype(F32) * gelu_slope(up_ref[:, gs])).astype(BF)

            n_c = fb // cw
            for c in range(n_c):
                cs = slice(c * cw, (c + 1) * cw)
                dh_s[:, cs] = dot_t(cot_s[...], wd_ref[cs, :]).astype(BF)
                if c > 0:
                    act(c - 1)
            for c in range(n_c):
                cs = slice(c * cw, (c + 1) * cw)
                for n in range(dim // nw):
                    ns = slice(n * nw, (n + 1) * nw)
                    acc_s[:, ns] += dot_t(dup_s[:, cs], wu_ref[ns, cs])
                if c == 0:
                    act(n_c - 1)
            return carry

        lax.fori_loop(0, n_blk, block, 0)
        pltpu.make_async_copy(x1_hbm, x_s, in_sem.at[3]).wait()

        @pl.when(i == 0)
        def _():
            wait(later)


        def rows_back(sl):
            x = x_s[sl, :].astype(F32)
            scale = scale_ref[n_layers - 1 - i, sl, 0:1]
            d_n = (acc_s[sl, :].astype(BF) + dng_s[sl, :]).astype(F32)
            acc_s[sl, :] = jnp.zeros((slab, dim), F32)
            proj = jnp.mean(d_n * x, axis=-1, keepdims=True)
            d_x = d_n * scale - x * (proj * (scale * scale * scale))
            cot_s[sl, :] = (cot_s[sl, :].astype(F32) + d_x).astype(BF)

        row_loop(tok, slab)(rows_back)
        proj_copy(i).wait()
        d_mixed = dot_t(cot_s[...], wp_s[...]).astype(BF)

        @pl.when(i == n_layers - 1)
        def _():
            dslots_s[...] = dot(slot_pick(n_emb * cap, slot_ref), d_mixed).astype(BF)

        wait(row_sends(i))

        @pl.when(i < n_layers - 1)
        def _():
            proj_copy(i + 1).start()
            gate_grads(gate_ref[jnp.maximum(n_layers - 2 - i, 0)], fet_ref[n_layers - 1 - i], d_mixed.astype(F32), rows_s, dgp_s)

        return carry

    lax.fori_loop(0, n_layers, one_layer, 0)
    start(mixed_sends)
    wait(gate_sends)
    wait(mixed_sends)


def order_rows(recv_ref, counts_ref, slot_bits, read_ref, write_ref, group_ref, meta_ref):
    n_dev, cap = recv_ref.shape
    shape = (n_dev, cap)
    square = (cap, cap)
    dev, lane = lax.broadcasted_iota(I32, shape, 0), lax.broadcasted_iota(I32, shape, 1)
    down, right = lax.broadcasted_iota(I32, square, 0), lax.broadcasted_iota(I32, square, 1)
    counts = counts_ref[:, 0:1]
    key = jnp.where(lane < counts, jnp.left_shift(recv_ref[...], slot_bits), 1 << 30) + dev * cap + lane

    def ones(cond):
        return jnp.where(cond, 1.0, 0.0)

    def digit(k):
        return jnp.bitwise_and(jnp.right_shift(key, 8 * k), 255).astype(F32).astype(BF)

    digits = [digit(k) for k in range(4)]
    same = ones(down == right).astype(BF)
    turned = sum(jnp.left_shift(dot_t(same, d).astype(I32), 8 * k) for k, d in enumerate(digits))
    rows = jnp.concatenate([d[None] for d in digits], axis=0)
    found = [jnp.zeros((8, cap), F32) for _ in range(n_dev)]
    for d in range(n_dev):
        column = turned[:, d:d + 1]
        smaller = sum(ones(key[e:e + 1, :] < column) for e in range(n_dev))
        rank = jnp.sum(smaller, axis=1, keepdims=True)
        mine = jnp.concatenate([rows[k, d:d + 1, :] for k in range(4)] * 2, axis=0)
        for w in range(n_dev):
            found[w] = found[w] + dot(mine, ones(rank - (w * cap) == right.astype(F32)).astype(BF))
    merged = [sum(jnp.left_shift(f[k:k + 1].astype(I32), 8 * k) for k in range(4)) for f in found]
    ordered = jnp.concatenate(merged, axis=0)

    before = pltpu.roll(ordered, 1, 1)
    before = jnp.where(lane == 0, pltpu.roll(before, 1, 0), before)
    after = pltpu.roll(ordered, cap - 1, 1)
    after = jnp.where(lane == cap - 1, pltpu.roll(after, n_dev - 1, 0), after)
    total = jnp.sum(counts_ref[...].astype(F32), axis=0, keepdims=True).astype(I32)
    place_in = dev * cap + lane
    live = place_in < total[:, 0:1]
    slot = jnp.bitwise_and(ordered, (1 << slot_bits) - 1)
    row = jnp.right_shift(ordered, slot_bits)
    group = jnp.right_shift(ordered, slot_bits + 3)
    begin, end = place_in == 0, place_in == n_dev * cap - 1
    same_row = jnp.logical_and(row == jnp.right_shift(before, slot_bits), jnp.logical_not(begin))
    fresh = jnp.logical_or(group != jnp.right_shift(before, slot_bits + 3), begin)
    last = jnp.logical_and(jnp.logical_or(group != jnp.right_shift(after, slot_bits + 3), end), live)
    place = dot(ones(fresh).astype(BF), ones(down <= right).astype(BF)).astype(I32)
    place = place - place[:, 0:1]
    read_ref[...] = jnp.right_shift(slot, 3) * 16 + jnp.bitwise_and(slot, 7) + jnp.where(same_row, -(1 << 31), 0)
    write_ref[...] = place * 16 + jnp.bitwise_and(row, 7)
    group_ref[...] = jnp.where(live, group, 0)
    n_out = jnp.sum(ones(last), axis=1, keepdims=True).astype(I32)
    goes_on = jnp.where(jnp.logical_and(jnp.logical_not(fresh), live), 1, 0)[:, 0:1]
    meta_lane = lax.broadcasted_iota(I32, meta_ref.shape, 1)
    meta = jnp.where(meta_lane == 0, n_out, jnp.where(meta_lane == 1, place[:, cap - 1:cap], goes_on))
    meta_ref[...] = jnp.where(meta_lane == 3, total, meta)


def scatter_kernel(cfg, read_ref, write_ref, group_ref, meta_ref, rows_hbm, gate_hbm, mixed_hbm, dt_in, dt_out,
                   rows_ref, gate_ref, mixed_ref, groups, prod, zero_s, spots, sems, in_sem, z_sem):
    unroll, bulk, z_first, z_chunks = cfg
    n_layers, window = groups.shape[1:3]
    n_slots = mixed_ref.shape[0]
    n_win = n_slots // window
    z_rows = zero_s.shape[0]
    count = meta_ref[0, 3]
    loads = [pltpu.make_async_copy(src, dst, in_sem.at[k]) for k, (src, dst) in enumerate(
        ((gate_hbm, gate_ref), (mixed_hbm, mixed_ref), (rows_hbm, rows_ref)))]
    start(loads)
    clear_rows(zero_s)

    def z_copy(c):
        return pltpu.make_async_copy(zero_s, dt_out.at[0, pl.ds(c * z_rows, z_rows)], z_sem.at[c])

    def z_start(c, carry):
        z_copy(c).start()
        return carry

    def z_wait(c, carry):
        z_copy(c).wait()
        return carry

    lax.fori_loop(z_first, z_chunks, z_start, 0)
    wait(loads[:2])

    def product(i, carry):
        step = 64
        mixed = mixed_ref[pl.ds(pl.multiple_of(i * step, step), step), :].astype(F32)
        for h in range(2):
            at = pl.ds(i * (step // 8), step // 8)
            prod[at, h] = gate_ref[at, h] * mixed[:, h * 128:(h + 1) * 128].reshape(step // 8, 8, 128)
        return carry

    lax.fori_loop(0, n_slots // 64, product, 0, unroll=4)

    def move(buf, spot, group, n):
        return pltpu.make_async_copy(groups.at[buf, :, pl.ds(spot, n)], dt_out.at[:, pl.ds(group, n)], sems.at[buf])

    def each(n, k, body):
        def trip(t, carry):
            for i in range(k):
                body(t * k + i)
            return carry

        def one(i, carry):
            body(i)
            return carry

        full = n // k
        lax.fori_loop(0, full, trip, 0)
        lax.fori_loop(full * k, n, one, 0)

    def settle(w):
        n = meta_ref[w, 0]

        def drain_bulk(j, carry):
            move(w % 2, 0, 0, bulk).wait()
            return carry

        def drain(j, carry):
            move(w % 2, 0, 0, 1).wait()
            return carry

        lax.fori_loop(0, n // bulk, drain_bulk, 0)
        lax.fori_loop(0, lax.rem(n, bulk), drain, 0)

    blank = jnp.zeros(groups.shape[3:], F32)
    accs = tuple(jnp.zeros((2, 128), F32) for _ in range(n_layers))
    z_done = jnp.int32(z_first)
    for w in range(n_win):
        buf = w % 2
        if w >= 2:
            settle(w - 2)
        left = jnp.clip(count - w * window, 0, window)
        trips = (left + (unroll - 1)) // unroll
        n_out = meta_ref[w, 0]

        def clear(u, buf=buf):
            for l in range(n_layers):
                groups[buf, l, u] = blank

        each(jnp.where(left > 0, jnp.minimum(n_out + 1, window), 0), 4, clear)
        if w == 0:
            wait(loads[2:])
        else:
            @pl.when(meta_ref[w, 2] > 0)
            def _(w=w, buf=buf):
                for l in range(n_layers):
                    groups[buf, l, 0] = groups[1 - buf, l, meta_ref[w - 1, 1]]

        sums = [groups.at[buf, l].reshape(window * 16, 128) for l in range(n_layers)]
        rows = [prod.reshape(n_slots * 2, 128)] + [rows_ref.at[l] for l in range(n_layers - 1)]

        def add(t, accs, w=w, sums=sums, rows=rows):
            for k in range(unroll):
                j = t * unroll + k
                word = read_ref[w, j]
                at = jnp.bitwise_and(word, n_slots * 2 - 1)
                same = word < 0
                to = write_ref[w, j]
                spots[jnp.right_shift(to, 4)] = group_ref[w, j]
                accs = tuple(jnp.where(same, acc, 0.0) + src[pl.ds(at, 2, stride=8), :] for acc, src in zip(accs, rows))
                for acc, dst in zip(accs, sums):
                    dst[pl.ds(to, 2, stride=8), :] = acc
            return accs

        accs = lax.fori_loop(0, trips, add, accs)
        need = jnp.where(n_out > 0, spots[jnp.maximum(n_out - 1, 0)] // z_rows + 1, z_done)
        need = jnp.maximum(need, z_done)
        lax.fori_loop(z_done, need, z_wait, 0)
        z_done = need
        each(n_out, 4, lambda u, buf=buf: move(buf, u, spots[u], 1).start())
    lax.fori_loop(z_done, z_chunks, z_wait, 0)
    for w in range(max(n_win - 2, 0), n_win):
        settle(w)


def solution(mesh):
    n_emb, n_dp = mesh.shape['emb'], mesh.shape['dp']
    n_dev = n_emb * n_dp
    tok_spec = P(('dp', 'emb'))
    act_spec = P(('dp', 'emb'), None)
    table_spec = P(None, 'emb', None)
    full_spec = P(None, None, None)
    hbm = pl.BlockSpec(memory_space=pl.ANY)
    vm = pl.BlockSpec(memory_space=pltpu.VMEM)
    sm = pl.BlockSpec(memory_space=pltpu.SMEM)
    big = jnp.iinfo(jnp.int32).max

    def params(n_grid, **kw):
        return pltpu.CompilerParams(vmem_limit_bytes=VMEM_BYTES, dimension_semantics=('arbitrary',) * n_grid if n_grid else None, **kw)

    def device_body(tok_ids, resid_in, cot_out, tables, w_up, w_down, w_gate, w_proj):
        n_layers, range_rows, e_dim = tables.shape
        tok = tok_ids.shape[0]
        dim, ffn = w_up.shape[1:]
        n_slots, n_serve = n_dev * CAP, n_emb * CAP
        my_emb, my_dp = lax.axis_index('emb'), lax.axis_index('dp')

        lanes = 128
        per_dot, dots = 32, 2
        dma = pltpu.SemaphoreType.DMA
        _, recv_loc, counts, pick, slot_row, slot_col = pl.pallas_call(
            functools.partial(plan_kernel, (n_dp, n_emb, CAP, range_rows, per_dot)),
            out_shape=[jax.ShapeDtypeStruct(shape, I32) for shape in (
                (n_dev, tok // lanes, lanes), (n_dev, CAP), (n_dev, lanes), (n_serve, 1), (1, tok), (tok, 1))],
            in_specs=[vm], out_specs=[vm] * 6,
            scratch_shapes=[pltpu.VMEM((n_dev, tok), F32), dma((n_dev - 1,)), dma((n_dev - 1,))],
            compiler_params=pltpu.CompilerParams(collective_id=0, has_side_effects=True),
            name='plan',
        )(tok_ids.reshape(tok // lanes, lanes))
        slot_bits = (n_slots - 1).bit_length()
        tab_shape = (n_layers, range_rows // 8, e_dim // 128, 8, 128)
        z_rows = 167
        z_chunks = tab_shape[1] // z_rows
        z_first = 2 * z_chunks // 3
        words = [jax.ShapeDtypeStruct((n_dev, CAP), I32)] * 3 + [jax.ShapeDtypeStruct((n_dev, lanes), I32)]
        served, dtab, read_word, write_word, group_word, meta = pl.pallas_call(
            functools.partial(gather_kernel, (n_layers, n_emb, CAP, per_dot, dots, z_first, slot_bits)),
            out_shape=[jax.ShapeDtypeStruct((n_layers, n_serve, e_dim), BF), jax.ShapeDtypeStruct(tab_shape, F32)] + words,
            in_specs=[sm, sm, vm, vm, vm, hbm],
            out_specs=[vm, hbm, vm, vm, vm, vm],
            scratch_shapes=[pltpu.VMEM((n_layers, n_serve * 8, e_dim), BF), pltpu.VMEM((z_rows,) + tab_shape[2:], F32), dma((n_emb,)), dma],
            compiler_params=params(0),
            name='table_rows',
        )(recv_loc, counts, recv_loc, counts, pick, tables)

        fb = 1024
        n_blk = ffn // fb
        cw, nw, slab = 512, 512, 32
        n_back = n_layers - 1
        z_per = z_chunks // n_blk
        assert z_chunks * z_rows == tab_shape[1] and z_per * n_blk == z_chunks
        matmul_flops = 4 * tok * dim * ffn
        w_bufs = [pltpu.VMEM((2, dim, fb), BF), pltpu.VMEM((2, fb, dim), BF), pltpu.VMEM((dim, e_dim), BF), pltpu.VMEM((e_dim, dim), BF)]
        x1, gate0, fetched = pl.pallas_call(
            functools.partial(first_kernel, (n_dp, n_emb, CAP, n_blk, cw, nw, slab)),
            out_shape=[
                jax.ShapeDtypeStruct((tok, dim), BF),
                jax.ShapeDtypeStruct((1, tok, e_dim), F32),
                jax.ShapeDtypeStruct((n_layers, tok, e_dim), BF),
            ],
            in_specs=[hbm] * 7,
            out_specs=[hbm] * 3,
            scratch_shapes=[
                pltpu.VMEM((tok, dim), BF), pltpu.VMEM((tok, 1), I32), pltpu.VMEM((1, tok, e_dim), F32), pltpu.VMEM((n_layers, tok, e_dim), BF),
                pltpu.VMEM((tok, dim), BF), pltpu.VMEM((tok, dim), F32), pltpu.VMEM((tok, fb), BF), pltpu.VMEM((tok, fb), F32),
                pltpu.VMEM((n_layers, n_serve, e_dim), BF), *w_bufs,
                dma((4,)), dma((4,)), dma((2, 2)), dma, dma((n_emb - 1,)), dma((n_emb - 1,)),
            ],
            compiler_params=params(0, collective_id=1, has_side_effects=True),
            cost_estimate=pl.CostEstimate(flops=matmul_flops, bytes_accessed=100 << 20, transcendentals=0),
            name='first_layer',
        )(resid_in, slot_col, served, w_gate, w_proj, w_up, w_down)

        out, saved, ups, gates, rows, dgp, dtab, scales = pl.pallas_call(
            functools.partial(forward_kernel, (n_back, n_blk, cw, nw, slab, z_per, z_chunks)),
            out_shape=[
                jax.ShapeDtypeStruct((tok, dim), BF),
                jax.ShapeDtypeStruct((n_back - 1, tok, dim), BF),
                jax.ShapeDtypeStruct((n_back, tok, ffn), F32),
                jax.ShapeDtypeStruct((n_back, tok, e_dim), F32),
                jax.ShapeDtypeStruct((tok, e_dim), F32),
                jax.ShapeDtypeStruct((tok, e_dim), BF),
                jax.ShapeDtypeStruct(tab_shape, F32),
                jax.ShapeDtypeStruct((n_back, tok, lanes), F32),
            ],
            in_specs=[hbm] * 8,
            out_specs=[hbm] * 8,
            input_output_aliases={7: 6},
            scratch_shapes=[
                pltpu.VMEM((tok, dim), BF), pltpu.VMEM((tok, dim), BF), pltpu.VMEM((tok, dim), F32), pltpu.VMEM((tok, fb), BF),
                pltpu.VMEM((2, tok, fb), F32), pltpu.VMEM((z_rows,) + tab_shape[2:], F32),
                pltpu.VMEM((n_layers, tok, e_dim), BF), pltpu.VMEM((n_back, tok, e_dim), F32), pltpu.VMEM((tok, e_dim), F32),
                pltpu.VMEM((tok, e_dim), BF), pltpu.VMEM((n_back, tok, lanes), F32), *w_bufs,
                dma((4,)), dma((2, 2)), dma((2,)), dma((4,)), dma((z_per,)),
            ],
            compiler_params=params(0),
            cost_estimate=pl.CostEstimate(flops=n_back * matmul_flops, bytes_accessed=400 << 20, transcendentals=0),
            name='forward',
        )(x1, cot_out, fetched, w_gate, w_proj, w_up, w_down, dtab)

        got, got_gate, mixed0 = pl.pallas_call(
            functools.partial(backward_kernel, (n_back, n_blk, n_dp, n_emb, CAP, cw, nw, slab)),
            out_shape=[jax.ShapeDtypeStruct((n_back, n_slots // 8, e_dim // 128, 8, 128), F32), jax.ShapeDtypeStruct((n_slots // 8, e_dim // 128, 8, 128), F32),
                       jax.ShapeDtypeStruct((n_slots, e_dim), BF)],
            in_specs=[hbm] * 15,
            out_specs=[hbm, hbm, hbm],
            scratch_shapes=[
                pltpu.VMEM((tok, dim), BF), pltpu.VMEM((tok, dim), BF), pltpu.VMEM((tok, dim), F32), pltpu.VMEM((tok, fb), BF), pltpu.VMEM((tok, fb), BF),
                pltpu.VMEM((tok, dim), BF), pltpu.VMEM((n_serve // 8, e_dim // 128, 8, 128), F32), pltpu.VMEM((n_serve // 8, e_dim // 128, 8, 128), F32),
                pltpu.VMEM((n_serve, e_dim), BF), pltpu.VMEM((tok, e_dim), F32), pltpu.VMEM((tok, e_dim), BF), pltpu.VMEM((1, tok), I32),
                pltpu.VMEM((1, tok, e_dim), F32), pltpu.VMEM((n_back, tok, e_dim), F32), pltpu.VMEM((n_layers, tok, e_dim), BF),
                pltpu.VMEM((n_back, tok, lanes), F32), pltpu.VMEM((2, tok, fb), F32), *w_bufs,
                dma((11,)), dma((2, 2)), dma((2,)), dma((3, n_dev - 1)), dma((3,)), dma((n_back + 2, n_dev - 1)),
            ],
            compiler_params=params(0, collective_id=2, has_side_effects=True),
            cost_estimate=pl.CostEstimate(flops=n_back * matmul_flops, bytes_accessed=400 << 20, transcendentals=0),
            name='backward',
        )(cot_out, x1, saved, rows, dgp, slot_row, gate0, gates, fetched, scales, ups, w_up, w_down, w_gate, w_proj)

        dtab = pl.pallas_call(
            functools.partial(scatter_kernel, (8, 32, z_first, z_chunks)),
            out_shape=jax.ShapeDtypeStruct(dtab.shape, F32),
            in_specs=[sm, sm, sm, sm, hbm, hbm, hbm, hbm],
            out_specs=hbm,
            input_output_aliases={7: 0},
            scratch_shapes=[pltpu.VMEM((n_back, n_slots * 2, 128), F32), pltpu.VMEM((n_slots // 8,) + tab_shape[2:], F32),
                            pltpu.VMEM((n_slots, e_dim), BF), pltpu.VMEM((2, n_layers, CAP) + tab_shape[2:], F32),
                            pltpu.VMEM((n_slots // 8,) + tab_shape[2:], F32), pltpu.VMEM((z_rows,) + tab_shape[2:], F32),
                            pltpu.SMEM((CAP,), I32), dma((2,)), dma((3,)), dma((z_chunks,))],
            compiler_params=params(0),
            name='scatter',
        )(read_word, write_word, group_word, meta, got.reshape(n_back, n_slots * 2, 128), got_gate, mixed0, dtab)
        dtab = dtab.transpose(0, 1, 3, 2, 4).reshape(n_layers, range_rows, e_dim)
        return out, dtab

    return jax.shard_map(device_body, mesh=mesh, in_specs=(tok_spec, act_spec, act_spec, table_spec, full_spec, full_spec, full_spec, full_spec), out_specs=(act_spec, table_spec), check_vma=False)
```

profile of v0, /device:TPU:0, one launch (start us, length us, event | category | flops | bytes accessed | tf_op | source)
XLA Modules:
  0.0 515.8 jit_solution(9379653160292437132)
XLA Ops:
  0.6 9.3 %plan.1 = (s32[8,4,128]{2,1,0:T(4,128)}, s32[8,256]{1,0:T(8,128)}, s32[8,128]{1,0:T(8,128)}, s32[1024,1]{1,0:T(8,128)}, s32[1,512]{1,0:T(1,128)}, /*index=5*/s32[512,1]{1,0:T(8,128)}) custom-call(s32[4,128]{1,0:T(4,128)} %bitcast.6), custom_call_target="tpu_custom_call" | custom-call | tf_op jit(solution)/shard_map/plan/pallas_call | solution.py:860
  9.9 15.1 %table_rows.1 = (bf16[4,1024,256]{2,1,0:T(8,128)(2,1)}, f32[4,4008,2,8,128]{4,3,2,1,0:T(8,128)}, s32[8,256]{1,0:T(8,128)}, s32[8,256]{1,0:T(8,128)}, s32[8,256]{1,0:T(8,128)}, /*index=5*/s32[8,128]{1,0:T(8,128)}) custom-call(s32[8,256]{1,0:T(8,128)} %get-tuple-element.28.loc_ref.recv_ref, s32[8,128]{1,0:T(8,128)} %get-tuple-element.29.counts_ref.tally_ref, ...), custom_call_target="tpu_custom_call" | custom-call | tf_op jit(solution)/shard_map/table_rows/pallas_call | solution.py:875
  25.0 68.3 %first_layer.1 = (bf16[512,3072]{1,0:T(8,128)(2,1)}, f32[1,512,256]{2,1,0:T(8,128)}, bf16[4,512,256]{2,1,0:T(8,128)(2,1)}) custom-call(bf16[512,3072]{1,0:T(8,128)(2,1)} %x_hbm.1, s32[512,1]{1,0:T(8,128)} %get-tuple-element.27.slot_hbm, bf16[4,1024,256]{2,1,0:T(8,128)(2,1)} %get-tuple-element.31.served_hbm, bf16[4,3072,256]{2,1,0:T(8,128)(2,1)} %wg_hbm.5, ...), custom_call_target="tpu_custom_call" | custom-call | flops 51539607552 | bytes 104857600 | tf_op jit(solution)/shard_map/first_layer/pallas_call | solution.py:893
  93.3 189.2 %forward.1 = (bf16[512,3072]{1,0:T(8,128)(2,1)}, bf16[2,512,3072]{2,1,0:T(8,128)(2,1)}, f32[3,512,8192]{2,1,0:T(8,128)}, f32[3,512,256]{2,1,0:T(8,128)}, f32[512...) custom-call(bf16[512,3072]{1,0:T(8,128)(2,1)} %get-tuple-element.32., ...), custom_call_target="tpu_custom_call", output_to_operand_aliasing={{6}: (7, {})} | custom-call | flops 154618822656 | bytes 419430400 | tf_op jit(solution)/shard_map/forward/pallas_call | solution.py:913
  282.6 210.0 %backward.1 = (f32[3,256,2,8,128]{4,3,2,1,0:T(8,128)}, f32[256,2,8,128]{3,2,1,0:T(8,128)}, bf16[2048,256]{1,0:T(8,128)(2,1)}) custom-call(bf16[512,3072]{1,0:T(8,128)(2,1)} %cot_hbm.3, bf16[512,3072]{1,0:T(8,128)(2,1)} %get-tuple-element.32.x_hbm.x1_hbm, bf16[2,512,3072]{2,1,0:T(8,128)(2,1)} %get-tuple-element.40.saved_hbm, ...), custom_call_target="tpu_custom_call" | custom-call | flops 154618822656 | bytes 419430400 | tf_op jit(solution)/shard_map/backward/pallas_call | solution.py:940
  492.5 23.1 %scatter.1 = f32[4,4008,2,8,128]{4,3,2,1,0:T(8,128)} custom-call(s32[8,256]{1,0:T(8,128)} %get-tuple-element.36.read_ref, s32[8,256]{1,0:T(8,128)} %get-tuple-element.37.write_ref, s32[8,256]{1,0:T(8,128)} %get-tuple-element.38.group_ref, s32[8,128]{1,0:T(8,128)} %get-tuple-element.39.meta_ref, ...), custom_call_target="tpu_custom_call", output_to_operand_aliasing={{}: (7, {})} | custom-call | tf_op jit(solution)/shard_map/scatter/pallas_call | solution.py:959
where the time goes:
time: 517 us; the launch traced here: 516 us
  Pallas kernels  515 us (100%)
    pallas_call x1, Pallas kernels, device_body(): pl.pallas_call(functools.partial(backward_kernel, (n_back, n_blk, n_dp, n...  210 us
    pallas_call x1, Pallas kernels, device_body(): pl.pallas_call(functools.partial(forward_kernel, (n_back, n_blk, cw, nw,...  189 us
    pallas_call x1, Pallas kernels, device_body(): pl.pallas_call(functools.partial(first_kernel, (n_dp, n_emb, CAP, n_blk,...  68.3 us
    pallas_call x1, Pallas kernels, device_body(): pl.pallas_call(functools.partial(scatter_kernel, (8, 32, z_first, z_chunk...  23.1 us
    pallas_call x1, Pallas kernels, device_body(): pl.pallas_call(functools.partial(gather_kernel, (n_layers, n_emb, CAP, pe...  15.1 us

commit v1 on v0

--- a/solution.py
+++ b/solution.py
@@ -330,9 +330,9 @@
     wait(outs)
 
 
-def forward_kernel(cfg, x_hbm, cot_hbm, fet_hbm, wg_hbm, wp_hbm, wu_hbm, wd_hbm, dt_in,
-                   out_hbm, saved_hbm, ups_hbm, gate_hbm, rows_hbm, dgp_hbm, dtab_hbm, scale_hbm,
-                   x_s, u_s, acc_s, h_s, up_s, zero_s, fet_ref, gate_ref, rows_ref, dgp_ref, scale_ref, wu_s, wd_s, wg_s, wp_s,
+def forward_kernel(cfg, x_hbm, fet_hbm, wg_hbm, wp_hbm, wu_hbm, wd_hbm, dt_in,
+                   out_hbm, saved_hbm, ups_hbm, gate_hbm, dtab_hbm, scale_hbm,
+                   x_s, u_s, acc_s, h_s, up_s, zero_s, fet_ref, gate_ref, scale_ref, wu_s, wd_s, wg_s, wp_s,
                    in_sem, w_sem, up_sem, out_sem, z_sem):
     n_layers, n_blk, cw, nw, slab, z_per, z_chunks = cfg
     tok, dim = x_s.shape
@@ -431,16 +431,9 @@
             x_s[sl, :] = x_new
             norm_rows(x_new.astype(F32), sl, u_s, acc_s, scale_ref.at[jnp.minimum(layer + 1, n_layers - 1)])
 
-        def last_rows(sl):
-            x_s[sl, :] = acc_s[sl, :].astype(BF)
-
         @pl.when(layer < n_layers - 1)
         def _():
             row_loop(tok, slab)(next_rows)
-
-        @pl.when(layer == n_layers - 1)
-        def _():
-            row_loop(tok, slab)(last_rows)
 
         @pl.when(layer < n_layers - 1)
         def _():
@@ -450,21 +443,22 @@
         return carry
 
     lax.fori_loop(0, n_layers, one_layer, 0)
-    put = pltpu.make_async_copy(x_s, out_hbm, out_sem.at[0])
-    put.start()
-    get = pltpu.make_async_copy(cot_hbm, u_s, in_sem.at[0])
-    get.start()
+    outs = []
+    for half in range(2):
+        rows = pl.ds(half * (tok // 2), tok // 2)
+
+        def last_rows(sl, half=half):
+            sl = pl.ds(sl.start + half * (tok // 2), slab)
+            x_s[sl, :] = acc_s[sl, :].astype(BF)
+
+        row_loop(tok // 2, slab)(last_rows)
+        outs.append(pltpu.make_async_copy(x_s.at[rows], out_hbm.at[rows], out_sem.at[2 * half]))
+        outs[-1].start()
     wait(z_copies(n_steps - 1))
     up_copy(0, 0, 0).wait()
     up_copy(0, 0, 1).wait()
-    get.wait()
-    d_mixed = dot_t(u_s[...], wp_s[...]).astype(BF).astype(F32)
-    gate_grads(gate_ref[n_layers - 1], fet_ref[n_layers], d_mixed, rows_ref, dgp_ref)
-    small = [pltpu.make_async_copy(rows_ref, rows_hbm, out_sem.at[2]), pltpu.make_async_copy(dgp_ref, dgp_hbm, out_sem.at[3])]
-    start(small)
     put_scales.wait()
-    put.wait()
-    wait(small)
+    wait(outs)
 
 
 def gate_grads(gate_pre, fetched, d_mixed, rows_ref, dgp_ref):
@@ -488,7 +482,7 @@
     return (lax.broadcasted_iota(I32, (n, slot_ref.shape[1]), 0) == slot_ref[...]).astype(BF)
 
 
-def backward_kernel(cfg, cot_hbm, x1_hbm, saved_hbm, rows_hbm, dgp_hbm, slot_hbm, gate0_hbm, gates_hbm, fet_hbm, scale_hbm,
+def backward_kernel(cfg, cot_hbm, x1_hbm, saved_hbm, slot_hbm, gate0_hbm, gates_hbm, fet_hbm, scale_hbm,
                     ups_hbm, wu_hbm, wd_hbm, wg_hbm, wp_hbm,
                     got_hbm, gate_hbm, mixed_hbm,
                     cot_s, x_s, acc_s, dup_s, dh_s, dng_s, slots_s, gslots_s, dslots_s, rows_s, dgp_s, slot_ref, gate0_ref, gate_ref, fet_ref, scale_ref, up_s, wu_s, wd_s, wg_s, wp_s,
@@ -542,15 +536,18 @@
         return pltpu.make_async_copy(saved_hbm.at[n_layers - 2 - i], x_s, in_sem.at[3])
 
     fetch = pltpu.make_async_copy(cot_hbm, cot_s, in_sem.at[0])
+    top = n_layers - 1
     soon = [pltpu.make_async_copy(src, dst, in_sem.at[4 + k]) for k, (src, dst) in enumerate(
-        ((gate0_hbm, gate0_ref), (slot_hbm, slot_ref), (rows_hbm, rows_s), (dgp_hbm, dgp_s)))]
+        ((gate0_hbm, gate0_ref), (slot_hbm, slot_ref), (gates_hbm.at[top], gate_ref.at[top]), (fet_hbm.at[top + 1], fet_ref.at[top + 1])))]
     later = [pltpu.make_async_copy(src, dst, in_sem.at[8 + k]) for k, (src, dst) in enumerate(
-        ((gates_hbm, gate_ref), (fet_hbm, fet_ref), (scale_hbm, scale_ref)))]
-    start(soon)
+        ((gates_hbm.at[pl.ds(0, top)], gate_ref.at[pl.ds(0, top)]), (fet_hbm.at[pl.ds(0, top + 1)], fet_ref.at[pl.ds(0, top + 1)]),
+         (scale_hbm, scale_ref)))]
+    start(soon[:2])
+    fetch.start()
+    proj_copy(-1).start()
+    start(soon[2:])
     gate_copy(0).start()
-    fetch.start()
     start(load(0, 0))
-    proj_copy(0).start()
     start(later)
 
     def clear(sl):
@@ -558,8 +555,13 @@
 
     row_loop(tok, slab)(clear)
     meet(peers)
-    wait(soon)
+    wait(soon[:2])
     to_slots(gelu(gate0_ref[0]), slot_ref, gslots_s)
+    fetch.wait()
+    proj_copy(-1).wait()
+    wait(soon[2:])
+    gate_grads(gate_ref[n_layers - 1], fet_ref[n_layers], dot_t(cot_s[...], wp_s[...]).astype(BF).astype(F32), rows_s, dgp_s)
+    proj_copy(0).start()
 
     def one_layer(i, carry):
         @pl.when(i < n_layers - 1)
@@ -584,7 +586,6 @@
         @pl.when(i == 0)
         def _():
             start(gate_sends)
-            fetch.wait()
 
         def block(f, carry):
             step = i * n_blk + f
@@ -714,30 +715,15 @@
 
 
 def scatter_kernel(cfg, read_ref, write_ref, group_ref, meta_ref, rows_hbm, gate_hbm, mixed_hbm, dt_in, dt_out,
-                   rows_ref, gate_ref, mixed_ref, groups, prod, zero_s, spots, sems, in_sem, z_sem):
-    unroll, bulk, z_first, z_chunks = cfg
+                   rows_ref, gate_ref, mixed_ref, groups, prod, spots, sems, in_sem):
+    unroll, bulk = cfg
     n_layers, window = groups.shape[1:3]
     n_slots = mixed_ref.shape[0]
     n_win = n_slots // window
-    z_rows = zero_s.shape[0]
     count = meta_ref[0, 3]
     loads = [pltpu.make_async_copy(src, dst, in_sem.at[k]) for k, (src, dst) in enumerate(
         ((gate_hbm, gate_ref), (mixed_hbm, mixed_ref), (rows_hbm, rows_ref)))]
     start(loads)
-    clear_rows(zero_s)
-
-    def z_copy(c):
-        return pltpu.make_async_copy(zero_s, dt_out.at[0, pl.ds(c * z_rows, z_rows)], z_sem.at[c])
-
-    def z_start(c, carry):
-        z_copy(c).start()
-        return carry
-
-    def z_wait(c, carry):
-        z_copy(c).wait()
-        return carry
-
-    lax.fori_loop(z_first, z_chunks, z_start, 0)
     wait(loads[:2])
 
     def product(i, carry):
@@ -783,7 +769,6 @@
 
     blank = jnp.zeros(groups.shape[3:], F32)
     accs = tuple(jnp.zeros((2, 128), F32) for _ in range(n_layers))
-    z_done = jnp.int32(z_first)
     for w in range(n_win):
         buf = w % 2
         if w >= 2:
@@ -822,12 +807,7 @@
             return accs
 
         accs = lax.fori_loop(0, trips, add, accs)
-        need = jnp.where(n_out > 0, spots[jnp.maximum(n_out - 1, 0)] // z_rows + 1, z_done)
-        need = jnp.maximum(need, z_done)
-        lax.fori_loop(z_done, need, z_wait, 0)
-        z_done = need
-        each(n_out, 4, lambda u, buf=buf: move(buf, u, spots[u], 1).start())
-    lax.fori_loop(z_done, z_chunks, z_wait, 0)
+        each(n_out, 8, lambda u, buf=buf: move(buf, u, spots[u], 1).start())
     for w in range(max(n_win - 2, 0), n_win):
         settle(w)
 
@@ -870,10 +850,9 @@
         tab_shape = (n_layers, range_rows // 8, e_dim // 128, 8, 128)
         z_rows = 167
         z_chunks = tab_shape[1] // z_rows
-        z_first = 2 * z_chunks // 3
         words = [jax.ShapeDtypeStruct((n_dev, CAP), I32)] * 3 + [jax.ShapeDtypeStruct((n_dev, lanes), I32)]
         served, dtab, read_word, write_word, group_word, meta = pl.pallas_call(
-            functools.partial(gather_kernel, (n_layers, n_emb, CAP, per_dot, dots, z_first, slot_bits)),
+            functools.partial(gather_kernel, (n_layers, n_emb, CAP, per_dot, dots, z_chunks, slot_bits)),
             out_shape=[jax.ShapeDtypeStruct((n_layers, n_serve, e_dim), BF), jax.ShapeDtypeStruct(tab_shape, F32)] + words,
             in_specs=[sm, sm, vm, vm, vm, hbm],
             out_specs=[vm, hbm, vm, vm, vm, vm],
@@ -910,38 +889,35 @@
             name='first_layer',
         )(resid_in, slot_col, served, w_gate, w_proj, w_up, w_down)
 
-        out, saved, ups, gates, rows, dgp, dtab, scales = pl.pallas_call(
+        out, saved, ups, gates, dtab, scales = pl.pallas_call(
             functools.partial(forward_kernel, (n_back, n_blk, cw, nw, slab, z_per, z_chunks)),
             out_shape=[
                 jax.ShapeDtypeStruct((tok, dim), BF),
                 jax.ShapeDtypeStruct((n_back - 1, tok, dim), BF),
                 jax.ShapeDtypeStruct((n_back, tok, ffn), F32),
                 jax.ShapeDtypeStruct((n_back, tok, e_dim), F32),
-                jax.ShapeDtypeStruct((tok, e_dim), F32),
-                jax.ShapeDtypeStruct((tok, e_dim), BF),
                 jax.ShapeDtypeStruct(tab_shape, F32),
                 jax.ShapeDtypeStruct((n_back, tok, lanes), F32),
             ],
-            in_specs=[hbm] * 8,
-            out_specs=[hbm] * 8,
-            input_output_aliases={7: 6},
+            in_specs=[hbm] * 7,
+            out_specs=[hbm] * 6,
+            input_output_aliases={6: 4},
             scratch_shapes=[
                 pltpu.VMEM((tok, dim), BF), pltpu.VMEM((tok, dim), BF), pltpu.VMEM((tok, dim), F32), pltpu.VMEM((tok, fb), BF),
                 pltpu.VMEM((2, tok, fb), F32), pltpu.VMEM((z_rows,) + tab_shape[2:], F32),
-                pltpu.VMEM((n_layers, tok, e_dim), BF), pltpu.VMEM((n_back, tok, e_dim), F32), pltpu.VMEM((tok, e_dim), F32),
-                pltpu.VMEM((tok, e_dim), BF), pltpu.VMEM((n_back, tok, lanes), F32), *w_bufs,
+                pltpu.VMEM((n_layers, tok, e_dim), BF), pltpu.VMEM((n_back, tok, e_dim), F32), pltpu.VMEM((n_back, tok, lanes), F32), *w_bufs,
                 dma((4,)), dma((2, 2)), dma((2,)), dma((4,)), dma((z_per,)),
             ],
             compiler_params=params(0),
             cost_estimate=pl.CostEstimate(flops=n_back * matmul_flops, bytes_accessed=400 << 20, transcendentals=0),
             name='forward',
-        )(x1, cot_out, fetched, w_gate, w_proj, w_up, w_down, dtab)
+        )(x1, fetched, w_gate, w_proj, w_up, w_down, dtab)
 
         got, got_gate, mixed0 = pl.pallas_call(
             functools.partial(backward_kernel, (n_back, n_blk, n_dp, n_emb, CAP, cw, nw, slab)),
             out_shape=[jax.ShapeDtypeStruct((n_back, n_slots // 8, e_dim // 128, 8, 128), F32), jax.ShapeDtypeStruct((n_slots // 8, e_dim // 128, 8, 128), F32),
                        jax.ShapeDtypeStruct((n_slots, e_dim), BF)],
-            in_specs=[hbm] * 15,
+            in_specs=[hbm] * 13,
             out_specs=[hbm, hbm, hbm],
             scratch_shapes=[
                 pltpu.VMEM((tok, dim), BF), pltpu.VMEM((tok, dim), BF), pltpu.VMEM((tok, dim), F32), pltpu.VMEM((tok, fb), BF), pltpu.VMEM((tok, fb), BF),
@@ -954,18 +930,17 @@
             compiler_params=params(0, collective_id=2, has_side_effects=True),
             cost_estimate=pl.CostEstimate(flops=n_back * matmul_flops, bytes_accessed=400 << 20, transcendentals=0),
             name='backward',
-        )(cot_out, x1, saved, rows, dgp, slot_row, gate0, gates, fetched, scales, ups, w_up, w_down, w_gate, w_proj)
+        )(cot_out, x1, saved, slot_row, gate0, gates, fetched, scales, ups, w_up, w_down, w_gate, w_proj)
 
         dtab = pl.pallas_call(
-            functools.partial(scatter_kernel, (8, 32, z_first, z_chunks)),
+            functools.partial(scatter_kernel, (8, 32)),
             out_shape=jax.ShapeDtypeStruct(dtab.shape, F32),
             in_specs=[sm, sm, sm, sm, hbm, hbm, hbm, hbm],
             out_specs=hbm,
             input_output_aliases={7: 0},
             scratch_shapes=[pltpu.VMEM((n_back, n_slots * 2, 128), F32), pltpu.VMEM((n_slots // 8,) + tab_shape[2:], F32),
                             pltpu.VMEM((n_slots, e_dim), BF), pltpu.VMEM((2, n_layers, CAP) + tab_shape[2:], F32),
-                            pltpu.VMEM((n_slots // 8,) + tab_shape[2:], F32), pltpu.VMEM((z_rows,) + tab_shape[2:], F32),
-                            pltpu.SMEM((CAP,), I32), dma((2,)), dma((3,)), dma((z_chunks,))],
+                            pltpu.VMEM((n_slots // 8,) + tab_shape[2:], F32), pltpu.SMEM((CAP,), I32), dma((2,)), dma((3,))],
             compiler_params=params(0),
             name='scatter',
         )(read_word, write_word, group_word, meta, got.reshape(n_back, n_slots * 2, 128), got_gate, mixed0, dtab)

time: 517 us -> 515 us (level)
  no operation moved by 1% of the time
where the time goes in v1:
time: 515 us; the launch traced here: 516 us
  Pallas kernels  515 us (100%)
    pallas_call x1, Pallas kernels, device_body(): pl.pallas_call(functools.partial(backward_kernel, (n_back, n_blk, n_dp, n...  210 us
    pallas_call x1, Pallas kernels, device_body(): pl.pallas_call(functools.partial(forward_kernel, (n_back, n_blk, cw, nw,...  185 us
    pallas_call x1, Pallas kernels, device_body(): pl.pallas_call(functools.partial(first_kernel, (n_dp, n_emb, CAP, n_blk,...  67.4 us
    pallas_call x1, Pallas kernels, device_body(): pl.pallas_call(functools.partial(scatter_kernel, (8, 32)), out_shape=jax....  23.1 us
    pallas_call x1, Pallas kernels, device_body(): pl.pallas_call(functools.partial(gather_kernel, (n_layers, n_emb, CAP, pe...  20 us

profile of v1, /device:TPU:0, one launch (start us, length us, event | category | flops | bytes accessed | tf_op | source)
XLA Modules:
  0.0 515.5 jit_solution(8185758175529867773)
XLA Ops:
  0.6 9.3 %plan.1 = (s32[8,4,128]{2,1,0:T(4,128)}, s32[8,256]{1,0:T(8,128)}, s32[8,128]{1,0:T(8,128)}, s32[1024,1]{1,0:T(8,128)}, s32[1,512]{1,0:T(1,128)}, /*index=5*/s32[512,1]{1,0:T(8,128)}) custom-call(s32[4,128]{1,0:T(4,128)} %bitcast.6), custom_call_target="tpu_custom_call" | custom-call | tf_op jit(solution)/shard_map/plan/pallas_call | solution.py:840
  9.9 20.0 %table_rows.1 = (bf16[4,1024,256]{2,1,0:T(8,128)(2,1)}, f32[4,4008,2,8,128]{4,3,2,1,0:T(8,128)}, s32[8,256]{1,0:T(8,128)}, s32[8,256]{1,0:T(8,128)}, s32[8,256]{1,0:T(8,128)}, /*index=5*/s32[8,128]{1,0:T(8,128)}) custom-call(s32[8,256]{1,0:T(8,128)} %get-tuple-element.26.loc_ref.recv_ref, s32[8,128]{1,0:T(8,128)} %get-tuple-element.27.counts_ref.tally_ref, ...), custom_call_target="tpu_custom_call" | custom-call | tf_op jit(solution)/shard_map/table_rows/pallas_call | solution.py:854
  29.9 67.4 %first_layer.1 = (bf16[512,3072]{1,0:T(8,128)(2,1)}, f32[1,512,256]{2,1,0:T(8,128)}, bf16[4,512,256]{2,1,0:T(8,128)(2,1)}) custom-call(bf16[512,3072]{1,0:T(8,128)(2,1)} %x_hbm.1, s32[512,1]{1,0:T(8,128)} %get-tuple-element.25.slot_hbm, bf16[4,1024,256]{2,1,0:T(8,128)(2,1)} %get-tuple-element.29.served_hbm, bf16[4,3072,256]{2,1,0:T(8,128)(2,1)} %wg_hbm.5, ...), custom_call_target="tpu_custom_call" | custom-call | flops 51539607552 | bytes 104857600 | tf_op jit(solution)/shard_map/first_layer/pallas_call | solution.py:872
  97.3 184.9 %forward.1 = (bf16[512,3072]{1,0:T(8,128)(2,1)}, bf16[2,512,3072]{2,1,0:T(8,128)(2,1)}, f32[3,512,8192]{2,1,0:T(8,128)}, f32[3,512,256]{2,1,0:T(8,128)}, f32[4,4...) custom-call(bf16[512,3072]{1,0:T(8,128)(2,1)} %get-tuple-element.30.x_hbm.x1_hbm, ...), custom_call_target="tpu_custom_call", output_to_operand_aliasing={{4}: (6, {})} | custom-call | flops 154618822656 | bytes 419430400 | tf_op jit(solution)/shard_map/forward/pallas_call | solution.py:892
  282.2 210.0 %backward.1 = (f32[3,256,2,8,128]{4,3,2,1,0:T(8,128)}, f32[256,2,8,128]{3,2,1,0:T(8,128)}, bf16[2048,256]{1,0:T(8,128)(2,1)}) custom-call(bf16[512,3072]{1,0:T(8,128)(2,1)} %cot_hbm.1, bf16[512,3072]{1,0:T(8,128)(2,1)} %get-tuple-element.30.x_hbm.x1_hbm, bf16[2,512,3072]{2,1,0:T(8,128)(2,1)} %get-tuple-element.38.saved_hbm, ...), custom_call_target="tpu_custom_call" | custom-call | flops 154618822656 | bytes 419430400 | tf_op jit(solution)/shard_map/backward/pallas_call | solution.py:916
  492.2 23.1 %scatter.1 = f32[4,4008,2,8,128]{4,3,2,1,0:T(8,128)} custom-call(s32[8,256]{1,0:T(8,128)} %get-tuple-element.34.read_ref, s32[8,256]{1,0:T(8,128)} %get-tuple-element.35.write_ref, s32[8,256]{1,0:T(8,128)} %get-tuple-element.36.group_ref, s32[8,128]{1,0:T(8,128)} %get-tuple-element.37.meta_ref, ...), custom_call_target="tpu_custom_call", output_to_operand_aliasing={{}: (7, {})} | custom-call | tf_op jit(solution)/shard_map/scatter/pallas_call | solution.py:935
